TPU v7x, 32 devices: a whole 2x2x4 slice. The times are simulated.
32 devices in a mesh: dp: 4 (over y, core), lat: 4 (over z), chan: 2 (over x).
Axes of the slice: x: 2, y: 2, z: 4, core: 2. Of those that a mesh axis runs over, the one named last changes fastest.
Arguments:
- saved_input: bfloat16 [4, 16, 720, 1024], P('dp', None, 'lat', 'chan'), may hold values from -6 to 6
- grad_output: bfloat16 [4, 16, 720, 1024], P('dp', None, 'lat', 'chan'), may hold values from -6 to 6
- legendre: bfloat16 [16, 192, 720], P('lat'), may hold values from -0.21875 to 0.21875
- quad_weight: float32 [720], replicated, may hold values from 0.3 to 3
- mixing_weight: bfloat16 [192, 512, 1024], P('lat', None, 'chan'), may hold values from -0.375 to 0.375
Outputs:
- grad_weight: bfloat16 [192, 512, 1024], P('lat', 'dp', 'chan')
- grad_input: bfloat16 [4, 16, 720, 1024], P('dp', None, 'lat', 'chan')
All inputs are finite; a program needn't handle non-finite values.
Results may differ from a plain program's by a relative error of at most 0.014.
Values may be sent and summed in bfloat16 or wider, within the bound.
A program may use at most 192 MiB of HBM per device.

v0:
```python
import jax
import jax.numpy as jnp
from jax import lax
from jax.sharding import PartitionSpec as P

BF = jnp.bfloat16
F32 = jnp.float32


def lane_swap(width):
    row = lax.broadcasted_iota(jnp.int32, (width, width), 0)
    col = lax.broadcasted_iota(jnp.int32, (width, width), 1)
    up = (row == col + 1) & (col % 2 == 0)
    down = (col == row + 1) & (row % 2 == 0)
    return (up.astype(F32) - down.astype(F32)).astype(BF)


def to_planes(width):
    row = lax.broadcasted_iota(jnp.int32, (width, width), 0)
    col = lax.broadcasted_iota(jnp.int32, (width, width), 1)
    return ((row // 2 + (row % 2) * (width // 2)) == col).astype(BF)


def lanes(x, matrix):
    return jnp.einsum("...q,qp->...p", x, matrix, preferred_element_type=F32).astype(BF)


def shifted(x, axis, step):
    n = lax.axis_size(axis)
    return lax.ppermute(x, axis, [(i, (i + step) % n) for i in range(n)])


def pick(x, index):
    return lax.dynamic_index_in_dim(x, index, 0, keepdims=False)


def on_device(saved_input, grad_output, legendre, quad_weight, mixing_weight):
    local_lat = saved_input.shape[2]
    width = saved_input.shape[3]
    own_m, n_deg, n_lat = legendre.shape
    lat_size = lax.axis_size("lat")
    n_dp, n_chan = lax.axis_size("dp"), lax.axis_size("chan")
    my_dp, my_chan = lax.axis_index("dp"), lax.axis_index("chan")
    batch = saved_input.shape[0] * n_dp
    swap, planes = lane_swap(width), to_planes(width)

    share = 2 if own_m % 2 == 0 and n_dp % 2 == 0 else 1
    per = own_m // share
    half_of = my_dp % share
    orders = pick(legendre.reshape(share, per * n_deg, n_lat), half_of)
    by_lat = orders.T.reshape(lat_size, local_lat, per * n_deg)
    by_lat = lax.all_to_all(by_lat, "lat", split_axis=0, concat_axis=0, tiled=True)
    held = [by_lat]
    if share == 2:
        other = lax.ppermute(by_lat, "dp", [(i, i ^ 1) for i in range(n_dp)])
        first = half_of == 0
        held = [jnp.where(first, by_lat, other), jnp.where(first, other, by_lat)]
    held = [
        jnp.transpose(x.reshape(lat_size, local_lat, per, n_deg), (0, 2, 3, 1))
        for x in held
    ]
    table = jnp.concatenate(held, axis=1).reshape(lat_size * own_m, n_deg, local_lat)
    weights = lax.dynamic_slice_in_dim(
        quad_weight, lax.axis_index("lat") * local_lat, local_lat
    )
    analysis = (table.astype(F32) * weights[None, None, :]).astype(BF)

    def spectrum(tab, grid):
        part = jnp.einsum("mlj,bmjq->lbmq", tab, grid, preferred_element_type=F32)
        return lax.psum_scatter(part.astype(BF), "lat", scatter_dimension=0, tiled=True)

    grads = spectrum(table, grad_output)
    spectra = spectrum(analysis, saved_input)
    n_l, n_b, n_m = grads.shape[:3]
    rows = n_b * n_m

    flat = grads.reshape(n_l, rows, width)
    both = jnp.concatenate([flat, lanes(flat, swap)], axis=1)
    n_i = mixing_weight.shape[1]
    mine = n_i // n_chan
    split_weight = mixing_weight.reshape(n_l, n_chan, mine, width)
    terms = jnp.einsum("lrq,lciq->clri", both, split_weight, preferred_element_type=F32)
    terms = terms.astype(BF)
    total = pick(terms, my_chan).astype(F32)
    for step in range(1, n_chan):
        sent = pick(terms, (my_chan + step) % n_chan)
        total = total + shifted(sent, "chan", step).astype(F32)
    total = total.astype(BF)
    half = lanes_join(total.reshape(n_l, 2, rows, mine), planes)
    everyone = [flat] + [shifted(flat, "dp", step) for step in range(1, n_dp)]

    spectra, half, *everyone = lax.optimization_barrier((spectra, half, *everyone))
    spec_in = lax.all_gather(half, "lat", axis=0, tiled=True).reshape(-1, n_b, n_m, width)
    grad_input = jnp.einsum(
        "mlj,lbmq->bmjq", analysis, spec_in, preferred_element_type=F32
    ).astype(BF)

    block = n_i // n_dp
    size = min(block, mine)
    per_chan, per_block = mine // size, block // size
    planar = lanes(spectra.reshape(n_l, rows, width), planes)
    pieces = jnp.moveaxis(planar.reshape(n_l, rows, 2, per_chan, size), 3, 0)
    pieces = pieces.reshape(per_chan, n_l, rows, 2 * size)
    pieces = jnp.concatenate(
        [pieces] + [shifted(pieces, "chan", step) for step in range(1, n_chan)]
    )

    def piece(index):
        place = (my_chan - index // per_chan) % n_chan
        return pick(pieces, place * per_chan + index % per_chan)

    def block_of(owner):
        parts = [piece(owner * per_block + t) for t in range(per_block)]
        return jnp.stack(parts)

    ours = [block_of(my_dp)]
    for step in range(1, n_dp):
        ours.append(shifted(block_of((my_dp + step) % n_dp), "dp", step))
    left = jnp.stack(ours).reshape(n_dp, per_block, n_l, rows, 2, size)
    right = jnp.stack(everyone)
    right = jnp.stack([right, lanes(right, swap)])
    grad_weight = jnp.einsum(
        "dtlrpi,pdlrq->ltiq", left, right, preferred_element_type=F32
    ) / batch
    return (grad_weight.reshape(n_l, block, width).astype(BF), grad_input)


def lanes_join(parts, planes):
    n = parts.shape[-1]
    real = jnp.einsum("lri,qi->lrq", parts[:, 0], planes[:, :n], preferred_element_type=F32)
    imag = jnp.einsum("lri,qi->lrq", parts[:, 1], planes[:, n:], preferred_element_type=F32)
    return (real + imag).astype(BF)


def solution(mesh):
    in_specs = (
        P("dp", None, "lat", "chan"),
        P("dp", None, "lat", "chan"),
        P("lat", None, None),
        P(),
        P("lat", None, "chan"),
    )
    out_specs = (P("lat", "dp", "chan"), P("dp", None, "lat", "chan"))
    return jax.shard_map(
        on_device, mesh=mesh, in_specs=in_specs, out_specs=out_specs, check_vma=False
    )
```

profile of v0, /device:TPU:0, one launch (start us, length us, event | category | flops | bytes accessed | tf_op | source)
XLA Modules:
  0.0 256.2 jit_solution(12533947805916880893)
XLA Ops:
  7.2 1.3 constant_dynamic-slice_fusion.4
  8.5 1.0 copy.36
  9.5 2.0 reshape.78
  11.5 21.7 %all_to_all.5 = bf16[4,180,384]{2,1,0:T(8,128)(2,1)S(1)} all-to-all(bf16[4,180,384]{2,1,0:T(8,128)(2,1)} %reshape.78), channel_id=1, replica_groups=mesh['dp'=4,'lat'=4,'chan'=2] {'lat'}, dimensions={0} | all-to-all | bytes 1105920 | tf_op jit(solution)/shard_map/all_to_all | solution.py:52
  33.2 1.0 copy.37
  34.2 2.3 collective-permute-done
  36.5 2.2 broadcast_select_fusion.1
  38.7 2.3 reshape.79
  41.1 2.3 reshape.80
  43.4 3.0 %pad_maximum_fusion.2 = bf16[4,4,192,180]{2,1,3,0:T(4,128)(2,1)S(1)} fusion(bf16[4,2,192,180]{2,1,3,0:T(2,128)(2,1)} %bitcast.111, bf16[4,2,192,180]{2,1,3,0:T(2,128)(2,1)} %bitcast.110), kind=kLoop, calls=%fused_computation.32 | loop fusion | flops 2211840 | bytes 2211840 | tf_op jit(solution)/shard_map/concatenate | solution.py:62
  46.7 1.1 copy-done.2
  47.8 5.5 %convert_bitcast_fusion.1 = bf16[192,1,16,512]{3,0,2,1:T(8,128)(2,1)} fusion(bf16[16,192,180]{1,2,0:T(8,128)(2,1)S(1)} %bitcast.97, bf16[16,180,512]{2,0,1:T(8,128)(2,1)S(1)} %bitcast.95), kind=kOutput, calls=%fused_computation.9 | convolution fusion | flops 567803904 | bytes 7200768 | tf_op jit(solution)/shard_map/mlj,bmjq->lbmq/dot_general | solution.py:69
  53.4 0.9 dynamic_slice.24
  54.2 0.5 copy-done.3
  54.7 7.5 %convert_bitcast_fusion.2 = bf16[192,1,16,512]{3,0,2,1:T(8,128)(2,1)} fusion(bf16[16,180,512]{2,0,1:T(8,128)(2,1)} %bitcast.109, bf16[16,192,180]{1,2,0:T(8,128)(2,1)S(1)} %bitcast.99, f32[180]{0:T(256)S(1)} %dynamic_slice.24), kind=kOutput, calls=%fused_computation.10 | convolution fusion | flops 569462784 | bytes 7201488 | tf_op jit(solution)/shard_map/mlj,bmjq->lbmq/dot_general | solution.py:69
  62.5 50.6 %reduce-scatter.5.cloned.1.call-done = bf16[48,1,16,512]{3,0,2,1:T(8,128)(2,1)} async-done(((bf16[192,1,16,512]{3,0,2,1:T(8,128)(2,1)}), bf16[48,1,16,512]{3,0,2,1:T(8,128)(2,1)}) %reduce-scatter.5.cloned.1.call-update) | async-done | bytes 786448 | tf_op jit(solution)/shard_map/reduce_scatter | solution.py:70
  113.1 2.0 convolution_convert_fusion.1
  115.0 1.3 maximum_bitcast_fusion
  116.3 13.0 %convolution_convert_fusion = bf16[48,32,2,256]{3,1,2,0:T(8,128)(2,1)S(1)} fusion(bf16[48,2,256,512]{3,2,1,0:T(8,128)(2,1)} %bitcast.96, bf16[48,32,512,1]{2,0,1,3:T(8,128)(2,1)} %maximum_bitcast_fusion), kind=kOutput, calls=%fused_computation.17 | convolution fusion | flops 806092800 | bytes 28311552 | tf_op jit(solution)/shard_map/lrq,lciq->clri/dot_general | solution.py:82
  129.3 1.0 dynamic-slice_bitcast_fusion
  130.3 1.5 collective-permute-start.1
  131.8 0.7 fusion.26
  132.5 1.5 collective-permute-start.3
  134.0 1.4 collective-permute-start.4
  135.4 14.1 %collective-permute-done.1 = bf16[48,32,256]{2,1,0:T(8,128)(2,1)} collective-permute-done((bf16[48,32,256]{2,1,0:T(8,128)(2,1)}, bf16[48,32,256]{2,1,0:T(8,128)(2,1)}, u32[]{:S(2)}, u32[]{:S(2)}) %collective-permute-start.1) | collective-permute-done | bytes 786464 | tf_op jit(solution)/shard_map/ppermute | solution.py:30
  149.5 1.4 fusion.23
  151.4 1.3 add_convert_fusion
  152.6 23.0 %reduce-scatter.3.cloned.1.call-done = bf16[48,1,16,512]{3,0,2,1:T(8,128)(2,1)} async-done(((bf16[192,1,16,512]{3,0,2,1:T(8,128)(2,1)}), bf16[48,1,16,512]{3,0,2,1:T(8,128)(2,1)}) %reduce-scatter.3.cloned.1.call-update) | async-done | bytes 786448 | tf_op jit(solution)/shard_map/reduce_scatter | solution.py:70
  175.7 2.0 convolution_convert_fusion.2
  178.0 0.5 copy.89
  178.4 1.4 reshape.89
  179.8 1.5 collective-permute-start.5
  181.3 1.2 constant_dynamic-update-slice_fusion.1
  182.5 3.8 %convert_bitcast_fusion = bf16[1,4,48,16,512]{4,2,3,1,0:T(8,128)(2,1)S(1)} fusion(bf16[1,48,16,512]{3,1,2,0:T(8,128)(2,1)} %bitcast.32, bf16[1,48,16,512]{3,1,2,0:T(8,128)(2,1)} %bitcast.31, bf16[1,48,16,512]{3,1,2,0:T(8,128)(2,1)} %bitcast.30, bf16[1,48,16,512]{3,1,2,0:T(8,128)(2,1)S(1)} %bitcast.104, s32[512]{0:T(512)S(1)} %get-tuple-element.28, ...), kind=kOutput, calls=%fused_computation.8 | convolution fusion | flops 1620049920 | bytes 6298112 | tf_op jit(solution)/shard_map/...q,qp->...p/dot_general | solution.py:25
  186.3 12.7 %collective-permute-done.5 = bf16[2,48,16,256]{3,2,1,0:T(8,128)(2,1)} collective-permute-done((bf16[2,48,16,256]{3,2,1,0:T(8,128)(2,1)}, bf16[2,48,16,256]{3,2,1,0:T(8,128)(2,1)}, u32[]{:S(2)}, u32[]{:S(2)}) %collective-permute-start.5) | collective-permute-done | bytes 786464 | tf_op jit(solution)/shard_map/ppermute | solution.py:30
  199.0 1.2 constant_dynamic-update-slice_fusion
  200.2 1.0 constant_dynamic-slice_fusion.3
  201.2 1.5 collective-permute-start.7
  202.7 1.5 collective-permute-start.8
  204.2 2.0 fusion.31
  206.2 3.2 %pad_maximum_fusion = bf16[2,4,48,16,512]{4,2,3,1,0:T(8,128)(2,1)} fusion(bf16[1,4,48,16,512]{4,2,3,1,0:T(8,128)(2,1)S(1)} %convert_bitcast_fusion, bf16[1,4,48,16,512]{4,2,3,1,0:T(8,128)(2,1)S(1)} %fusion.31), kind=kLoop, calls=%fused_computation.2 | loop fusion | flops 3145728 | bytes 12582912 | tf_op jit(solution)/shard_map/stack | solution.py:121
  209.6 2.7 %collective-permute-done.6 = bf16[1,48,16,256]{3,2,1,0:T(8,128)(2,1)S(1)} collective-permute-done((bf16[1,48,16,256]{3,2,1,0:T(8,128)(2,1)}, bf16[1,48,16,256]{3,2,1,0:T(8,128)(2,1)S(1)}, u32[]{:S(2)}, u32[]{:S(2)}) %collective-permute-start.6) | collective-permute-done | bytes 393248 | tf_op jit(solution)/shard_map/ppermute | solution.py:30
  212.4 1.0 collective-permute-done.7
  213.6 6.8 %collective-permute-done.8 = bf16[1,48,16,256]{3,2,1,0:T(8,128)(2,1)S(1)} collective-permute-done((bf16[1,48,16,256]{3,2,1,0:T(8,128)(2,1)}, bf16[1,48,16,256]{3,2,1,0:T(8,128)(2,1)S(1)}, u32[]{:S(2)}, u32[]{:S(2)}) %collective-permute-start.8) | collective-permute-done | bytes 393248 | tf_op jit(solution)/shard_map/ppermute | solution.py:30
  220.6 13.5 %fusion = bf16[48,128,512]{2,1,0:T(8,128)(2,1)} fusion(bf16[2,4,48,16,512]{4,2,3,1,0:T(8,128)(2,1)} %pad_maximum_fusion, bf16[1,1,48,16,2,128]{5,3,4,2,0,1:T(8,128)(2,1)S(1)} %copy.51, bf16[1,1,48,16,2,128]{5,3,4,2,0,1:T(8,128)(2,1)S(1)} %copy.50, bf16[1,1,48,16,2,128]{5,3,4,2,0,1:T(8,128)(2,1)S(1)} %copy.49, bf16[1,1,48,16,2,128]{5,3,4,2,0,1:T(8,128)(2,1)S(1)} %copy.48), kind=kOutput, calls=%fused_computation.1 | convolution fusion | flops 813957120 | bytes 14155776 | tf_op jit(solution)/shard_map/dtlrpi,pdlrq->ltiq/dot_general | solution.py:122
  234.0 6.6 %all-gather.2.cloned.1.call-done = bf16[192,16,512]{2,1,0:T(8,128)(2,1)} async-done(((bf16[48,16,512]{2,1,0:T(8,128)(2,1)}), bf16[192,16,512]{2,1,0:T(8,128)(2,1)}) %all-gather.2.cloned.1.call-update) | async-done | bytes 3145744 | tf_op jit(solution)/shard_map/all_gather | solution.py:93
  240.7 6.4 %convert_bitcast_fusion.3 = bf16[1,16,180,512]{3,2,1,0:T(8,128)(2,1)S(1)} fusion(bf16[192,16,512]{2,1,0:T(8,128)(2,1)} %all-gather.2.cloned.1.call-done, bf16[16,192,180]{1,2,0:T(8,128)(2,1)} %bitcast.98, f32[180]{0:T(256)S(1)} %dynamic_slice.24), kind=kOutput, calls=%fused_computation.15 | convolution fusion | flops 569364480 | bytes 7201488 | tf_op jit(solution)/shard_map/mlj,lbmq->bmjq/dot_general | solution.py:94
  247.0 2.6 %copy.56 = bf16[1,16,180,512]{3,1,2,0:T(8,128)(2,1)} copy(bf16[1,16,180,512]{3,2,1,0:T(8,128)(2,1)S(1)} %convert_bitcast_fusion.3) | data formatting | bytes 5898240
  (36 shorter events, 1.9 us)
Async XLA Ops:
  7.2 39.5 %copy-start = (bf16[1,16,180,512]{3,1,2,0:T(8,128)(2,1)S(1)}, bf16[1,16,180,512]{3,1,2,0:T(8,128)(2,1)}, u32[]{:S(2)}) copy-start(bf16[1,16,180,512]{3,1,2,0:T(8,128)(2,1)} %param.6) | copy-start | bytes 8847364
  7.2 105.9 %reduce-scatter.5.cloned.1.call-start = ((), (), s32[]{:S(2)}) async-start(), calls=%async_computation.4 | async-start | bytes 3932160 | tf_op jit(solution)/shard_map/reduce_scatter | solution.py:70
  34.2 2.3 collective-permute-start
  46.7 1.1 copy-start.2
  53.3 1.4 copy-start.3
  53.3 122.4 %reduce-scatter.3.cloned.1.call-start = ((), (), s32[]{:S(2)}) async-start(), calls=%async_computation.3 | async-start | bytes 3932160 | tf_op jit(solution)/shard_map/reduce_scatter | solution.py:70
  62.2 178.5 %all-gather.2.cloned.1.call-start = ((), (), s32[]{:S(2)}) async-start(), calls=%async_computation.5 | async-start | bytes 3932160 | tf_op jit(solution)/shard_map/all_gather | solution.py:93
  113.1 2.0 copy-start.4
  130.3 19.2 %collective-permute-start.1 = (bf16[48,32,256]{2,1,0:T(8,128)(2,1)}, bf16[48,32,256]{2,1,0:T(8,128)(2,1)}, u32[]{:S(2)}, u32[]{:S(2)}) collective-permute-start(bf16[48,32,256]{2,1,0:T(8,128)(2,1)} %dynamic-slice_bitcast_fusion), channel_id=1, source_target_pairs={{0,1},{1,0},{2,3},{3,2},{4,5},{5,4},{6,7},{7,6},{8,9},{9,8},{10,11... | collective-permute-start | bytes 2359304 | tf_op jit(solution)/shard_map/ppermute | solution.py:30
  132.4 43.3 %collective-permute-start.2 = (bf16[48,16,512]{2,0,1:T(8,128)(2,1)S(1)}, bf16[48,16,512]{2,0,1:T(8,128)(2,1)}, u32[]{:S(2)}, u32[]{:S(2)}) collective-permute-start(bf16[48,16,512]{2,0,1:T(8,128)(2,1)S(1)} %bitcast.101), channel_id=1, source_target_pairs={{0,8},{8,16},{16,24},{24,0},{1,9},{9,17},{17,25},{25,1},{2,10},{10... | collective-permute-start | bytes 2359304 | tf_op jit(solution)/shard_map/ppermute | solution.py:30
  132.5 43.2 %collective-permute-start.3 = (bf16[48,16,512]{2,0,1:T(8,128)(2,1)S(1)}, bf16[48,16,512]{2,0,1:T(8,128)(2,1)}, u32[]{:S(2)}, u32[]{:S(2)}) collective-permute-start(bf16[48,16,512]{2,0,1:T(8,128)(2,1)S(1)} %bitcast.102), channel_id=1, source_target_pairs={{0,16},{8,24},{16,0},{24,8},{1,17},{9,25},{17,1},{25,9},{2,18},{10... | collective-permute-start | bytes 2359304 | tf_op jit(solution)/shard_map/ppermute | solution.py:30
  134.0 41.7 %collective-permute-start.4 = (bf16[48,16,512]{2,0,1:T(8,128)(2,1)S(1)}, bf16[48,16,512]{2,0,1:T(8,128)(2,1)}, u32[]{:S(2)}, u32[]{:S(2)}) collective-permute-start(bf16[48,16,512]{2,0,1:T(8,128)(2,1)S(1)} %bitcast.103), channel_id=1, source_target_pairs={{0,24},{8,0},{16,8},{24,16},{1,25},{9,1},{17,9},{25,17},{2,26},{10... | collective-permute-start | bytes 2359304 | tf_op jit(solution)/shard_map/ppermute | solution.py:30
  179.8 19.2 %collective-permute-start.5 = (bf16[2,48,16,256]{3,2,1,0:T(8,128)(2,1)}, bf16[2,48,16,256]{3,2,1,0:T(8,128)(2,1)}, u32[]{:S(2)}, u32[]{:S(2)}) collective-permute-start(bf16[2,48,16,256]{3,2,1,0:T(8,128)(2,1)} %reshape.89), channel_id=1, source_target_pairs={{0,1},{1,0},{2,3},{3,2},{4,5},{5,4},{6,7},{7,6},{8,9},{9,8},{10,11... | collective-permute-start | bytes 2359304 | tf_op jit(solution)/shard_map/ppermute | solution.py:30
  201.2 11.0 %collective-permute-start.6 = (bf16[1,48,16,256]{3,2,1,0:T(8,128)(2,1)}, bf16[1,48,16,256]{3,2,1,0:T(8,128)(2,1)S(1)}, u32[]{:S(2)}, u32[]{:S(2)}) collective-permute-start(bf16[1,48,16,256]{3,2,1,0:T(8,128)(2,1)} %get-tuple-element.23), channel_id=1, source_target_pairs={{0,8},{8,16},{16,24},{24,0},{1,9},{9,17},{17,25},{25,1},{2,10},{10... | collective-permute-start | bytes 1179656 | tf_op jit(solution)/shard_map/ppermute | solution.py:30
  201.2 12.2 %collective-permute-start.7 = (bf16[1,48,16,256]{3,2,1,0:T(8,128)(2,1)}, bf16[1,48,16,256]{3,2,1,0:T(8,128)(2,1)S(1)}, u32[]{:S(2)}, u32[]{:S(2)}) collective-permute-start(bf16[1,48,16,256]{3,2,1,0:T(8,128)(2,1)} %get-tuple-element.22), channel_id=1, source_target_pairs={{0,16},{8,24},{16,0},{24,8},{1,17},{9,25},{17,1},{25,9},{2,18},{10... | collective-permute-start | bytes 1179656 | tf_op jit(solution)/shard_map/ppermute | solution.py:30
  202.7 17.7 %collective-permute-start.8 = (bf16[1,48,16,256]{3,2,1,0:T(8,128)(2,1)}, bf16[1,48,16,256]{3,2,1,0:T(8,128)(2,1)S(1)}, u32[]{:S(2)}, u32[]{:S(2)}) collective-permute-start(bf16[1,48,16,256]{3,2,1,0:T(8,128)(2,1)} %get-tuple-element.21), channel_id=1, source_target_pairs={{0,24},{8,0},{16,8},{24,16},{1,25},{9,1},{17,9},{25,17},{2,26},{10... | collective-permute-start | bytes 1179656 | tf_op jit(solution)/shard_map/ppermute | solution.py:30
  240.7 9.0 %copy-start.1 = (bf16[1,16,180,512]{3,1,2,0:T(8,128)(2,1)S(1)}, bf16[1,16,180,512]{3,1,2,0:T(8,128)(2,1)}, u32[]{:S(2)}) copy-start(bf16[1,16,180,512]{3,1,2,0:T(8,128)(2,1)} %param.6) | copy-start | bytes 8847364
Sparse Core Ops, SparseCore 0:
  53.4 59.5 reduce-scatter.4
  115.4 60.2 reduce-scatter.2
  177.3 63.3 all-gather.1
where the time goes:
time: 257 us; the launch traced here: 256 us
  waiting for transfers between devices  120 us (47%)
  matrix products  55.3 us (22%)
  local copies, waits for them, and re-layouts  22.2 us (9%)
  blocking collectives  21.7 us (8%)
  between operations  14 us (5%)
  other arithmetic  13.9 us (5%)
  starting transfers between devices  9.19 us (4%)
    reduce_scatter x2, waiting for transfers between devices, spectrum(): lax.psum_scatter(part.astype(BF), 'lat', scatter_dimension=0, tiled=True)  73.7 us
    ppermute x8, waiting for transfers between devices, shifted(): return lax.ppermute(x, axis, [(i, (i + step) % n) for i in range(n)])  37.3 us
    all_to_all x1, blocking collectives, on_device(): lax.all_to_all(by_lat, 'lat', split_axis=0, concat_axis=0, tiled=True)  21.7 us
    dot_general x1, matrix products, on_device(): jnp.einsum('dtlrpi,pdlrq->ltiq', left, right, preferred_element_type=F32)  13.5 us
    dot_general x1, matrix products, on_device(): jnp.einsum('lrq,lciq->clri', both, split_weight, preferred_element_type=F32)  13 us
    dot_general x2, matrix products, spectrum(): part = jnp.einsum('mlj,bmjq->lbmq', tab, grid, preferred_element_type=F32)  13 us
    ppermute x8, starting transfers between devices, shifted(): return lax.ppermute(x, axis, [(i, (i + step) % n) for i in range(n)])  8.88 us
    dot_general x3, matrix products, lanes(): jnp.einsum('...q,qp->...p', x, matrix, preferred_element_type=F32)  7.75 us
  transfers between devices with their start and end apart: 12, of which 9 were waited for; matrix products, arithmetic and copies ran while one was open for 23% of the time, Pallas kernels for 0%

commit v1 on v0

--- a/solution.py
+++ b/solution.py
@@ -1,10 +1,673 @@
+import functools
 import jax
 import jax.numpy as jnp
 from jax import lax
+from jax.experimental import pallas as pl
+from jax.experimental.pallas import tpu as pltpu
 from jax.sharding import PartitionSpec as P
 
 BF = jnp.bfloat16
 F32 = jnp.float32
+MESH = pl.DeviceIdType.MESH
+
+
+def loop(n, body, unroll=1):
+    if n % unroll:
+        unroll = 1
+
+    def some(i, carry):
+        for j in range(unroll):
+            body(i * unroll + j)
+        return carry
+
+    lax.fori_loop(0, n // unroll, some, 0)
+
+
+def nn(a, b):
+    return lax.dot_general(a, b, (((1,), (0,)), ((), ())), preferred_element_type=F32)
+
+
+def nt(a, b):
+    return lax.dot_general(a, b, (((1,), (1,)), ((), ())), preferred_element_type=F32)
+
+
+def tn(a, b):
+    return lax.dot_general(a, b, (((0,), (0,)), ((), ())), preferred_element_type=F32)
+
+
+def put(ref, at, value):
+    for i in range(ref.shape[0]):
+        ref[i, at, :] = value[:, i * 128:(i + 1) * 128]
+
+
+def take(ref, start, size, stride):
+    at = pl.ds(start, size, stride=stride)
+    return jnp.concatenate([ref[i, at, :].astype(BF) for i in range(ref.shape[0])], axis=1)
+
+
+def partner_rows(x):
+    width = x.shape[-1]
+    lane = lax.broadcasted_iota(jnp.int32, x.shape, 1)
+    ahead, behind = pltpu.roll(x, width - 1, 1), pltpu.roll(x, 1, 1)
+    return jnp.where(lane % 2 == 0, ahead, -behind)
+
+
+def layer_kernel(
+    dims,
+    leg_hbm, quad_hbm, g_hbm, x_hbm, w_hbm,
+    gi_hbm, e_hbm, l_hbm,
+    leg, tab, quad, raw, wide, table, pg, ps, rgp, rgm, rsp, rsm,
+    tall, flat, keep, give, got, spec, planar, rows16, wbuf, split, join, outb,
+    load_sem, w_sem, zs_sem, zr_sem, xs_sem, xr_sem, cs_sem, cr_sem,
+    gps, gpr, gms, gmr, sps, spr, sms, smr,
+    ts_sem, tr_sem, aps, apr, ams, amr, es_sem, er_sem, el_sem, ps_sem, pr_sem, pl_sem, out_sem,
+):
+    J, M, Q, L, LB, OM, Z, NDP, NCH, K, KB, WL, WS = dims
+    half = Q // 2
+    z, c, d = lax.axis_index("lat"), lax.axis_index("chan"), lax.axis_index("dp")
+    core = d % 2
+    mate, other = d + 1 - 2 * core, 1 - c
+    per = OM // (2 * NCH)
+
+    def load(src, dst, i):
+        return pltpu.make_async_copy(src, dst, load_sem.at[i])
+
+    loads = [load(leg_hbm, leg, 0), load(g_hbm, raw.at[0], 1), load(x_hbm, raw.at[1], 2),
+             load(quad_hbm, quad, 3)]
+    for copy in loads:
+        copy.start()
+
+    def w_copy(i, slot):
+        return pltpu.make_async_copy(w_hbm.at[pl.ds(i * WL, WL)], wbuf.at[slot], w_sem.at[slot])
+
+    for i in range(WS):
+        w_copy(i, i).start()
+
+    barrier = pltpu.get_barrier_semaphore()
+    for i in range(1, Z):
+        pl.semaphore_signal(barrier, inc=1, device_id={"lat": (z + i) % Z}, device_id_type=MESH)
+    for i in range(NDP):
+        for j in range(NCH):
+            if i or j:
+                pl.semaphore_signal(
+                    barrier, inc=1, device_id={"dp": (d + i) % NDP, "chan": (c + j) % NCH},
+                    device_id_type=MESH)
+
+    loads[0].wait()
+
+    def cut(i):
+        whole = leg[i]
+        for t in range(Z):
+            tab[t, i] = whole[:, t * J:(t + 1) * J]
+
+    loop(OM, cut)
+
+    def own_table(i):
+        table[z * OM + i] = tab[z, i]
+
+    loop(OM, own_table)
+    loads[1].wait()
+    JB = 12 if J % 12 == 0 else 1
+
+    def spread(which):
+        def body(i):
+            block = raw[which, pl.ds(i * JB, JB)]
+            put(wide, pl.ds(i * JB * M, JB * M), block.astype(F32).reshape(JB * M, Q))
+        loop(J // JB, body)
+
+    def rows_of(m):
+        return take(wide, m, J, M)
+
+    spread(0)
+
+    def grad_part(m):
+        pg[m] = nn(table[m], rows_of(m)).astype(BF)
+
+    pl.semaphore_wait(barrier, Z - 1 + NDP * NCH - 1)
+
+    mine_q = c * 2 + core
+
+    def z_copy(target, source):
+        return pltpu.make_async_remote_copy(
+            src_ref=tab.at[target, pl.ds(mine_q * per, per)],
+            dst_ref=table.at[pl.ds(source * OM + mine_q * per, per)],
+            send_sem=zs_sem.at[target], recv_sem=zr_sem.at[source],
+            device_id={"lat": target}, device_id_type=MESH)
+
+    def quarter(owner, q, sends, recvs, where):
+        part = table.at[pl.ds(owner * OM + q * per, per)]
+        return pltpu.make_async_remote_copy(
+            src_ref=part, dst_ref=part, send_sem=sends, recv_sem=recvs,
+            device_id=where, device_id_type=MESH)
+
+    def line_steps(p, rp, rm, sends_p, recvs_p, sends_m, recvs_m, region):
+        def copy_p(s, t):
+            r = region(s, t)
+            return pltpu.make_async_remote_copy(
+                src_ref=p.at[r], dst_ref=rp.at[r], send_sem=sends_p.at[s, t],
+                recv_sem=recvs_p.at[s, t], device_id={"lat": (z + 1) % Z}, device_id_type=MESH)
+
+        def copy_m(s, t):
+            r = region(s, t)
+            return pltpu.make_async_remote_copy(
+                src_ref=p.at[r], dst_ref=rm.at[r], send_sem=sends_m.at[s, t],
+                recv_sem=recvs_m.at[s, t], device_id={"lat": (z + Z - 1) % Z}, device_id_type=MESH)
+
+        return copy_p, copy_m
+
+    def g_region(s, t):
+        return (pl.ds(s * OM, OM), pl.ds(t * LB, LB), slice(None))
+
+    def s_region(k, t):
+        return (slice(None), pl.ds(t * LB + k * KB, KB), slice(None))
+
+    g_p, g_m = line_steps(pg, rgp, rgm, gps, gpr, gms, gmr, g_region)
+    s_p, s_m = line_steps(ps, rsp, rsm, sps, spr, sms, smr, s_region)
+
+    def add_g(r, s, t):
+        def body(i):
+            at = (s * OM + i, pl.ds(t * LB, LB), slice(None))
+            pg[at] = (pg[at].astype(F32) + r[at].astype(F32)).astype(BF)
+        loop(OM, body)
+
+    def add_s(r, k, t):
+        def body(i):
+            at = (i, pl.ds(t * LB + k * KB, KB), slice(None))
+            ps[at] = (ps[at].astype(F32) + r[at].astype(F32)).astype(BF)
+        loop(M, body)
+
+    first, last = z == 0, z == Z - 1
+
+    for i in range(1, Z):
+        z_copy((z + Z - i) % Z, z).start()
+    loop(OM, lambda i: grad_part(z * OM + i))
+
+    @pl.when(first)
+    def _():
+        for t in range(Z - 1, 0, -1):
+            g_p(0, t).start()
+
+    @pl.when(last)
+    def _():
+        for t in range(Z - 1):
+            g_m(Z - 1, t).start()
+
+    for i in range(1, Z):
+        source = (z + i) % Z
+        z_copy(z, source).wait_recv()
+        quarter(source, mine_q, xs_sem.at[source], xr_sem.at[source], {"chan": other}).start()
+        quarter(source, mine_q, cs_sem.at[source, 0], cr_sem.at[source, 0], {"dp": mate}).start()
+    for i in range(1, Z):
+        source = (z + i) % Z
+        x_q = other * 2 + core
+        quarter(source, x_q, xs_sem.at[source], xr_sem.at[source], {"chan": other}).wait_recv()
+        quarter(source, x_q, cs_sem.at[source, 1], cr_sem.at[source, 1], {"dp": mate}).start()
+    for i in range(1, Z):
+        source = (z + i) % Z
+        quarter(source, c * 2 + 1 - core, cs_sem.at[source, 0], cr_sem.at[source, 0], {"dp": mate}).wait_recv()
+        quarter(source, other * 2 + 1 - core, cs_sem.at[source, 1], cr_sem.at[source, 1], {"dp": mate}).wait_recv()
+        loop(OM, lambda i: grad_part(source * OM + i))
+
+    def clear(r):
+        def body(i):
+            r[i, pl.ds(z * LB, LB), :] = jnp.zeros((LB, Q), BF)
+        loop(M, body)
+
+    @pl.when(first)
+    def _():
+        clear(rgp)
+        clear(rsp)
+
+    @pl.when(last)
+    def _():
+        clear(rgm)
+        clear(rsm)
+
+    def order(u):
+        v = u - (Z - 1)
+        early = u < Z - 1
+        return jnp.where(early, 0, 1 + v % (Z - 1)), jnp.where(early, Z - 1 - u, Z - 1 - v // (Z - 1))
+
+    pieces = Z * (Z - 1)
+
+    def g_ends(u):
+        s, t = order(u)
+
+        @pl.when(first)
+        def _():
+            g_p(s, t).start()
+
+        @pl.when(last)
+        def _():
+            g_m(Z - 1 - s, Z - 1 - t).start()
+
+    lax.fori_loop(Z - 1, pieces, lambda u, v: (g_ends(u), v)[1], 0)
+
+    def g_step(u):
+        s, t = order(u)
+        back, low = Z - 1 - s, Z - 1 - t
+
+        @pl.when((z > 0) & (t > z))
+        def _():
+            g_p(s, t).wait_recv()
+            add_g(rgp, s, t)
+            g_p(s, t).start()
+
+        @pl.when((z < Z - 1) & (low < z))
+        def _():
+            g_m(back, low).wait_recv()
+            add_g(rgm, back, low)
+            g_m(back, low).start()
+
+    loop(Z - 1, g_step)
+
+    loads[2].wait()
+    loads[3].wait()
+    spread(1)
+
+    def input_part(m):
+        tall[m] = (table[m].astype(F32) * quad[pl.ds(z, 1), :]).astype(BF)
+        ps[m] = nn(tall[m], rows_of(m)).astype(BF)
+
+    loop(M, input_part, 2)
+
+    def s_send(k):
+        @pl.when(first)
+        def _():
+            for t in range(Z - 1, 0, -1):
+                s_p(k, t).start()
+
+        @pl.when(last)
+        def _():
+            for t in range(Z - 1):
+                s_m(k, t).start()
+
+    s_send(0)
+    lax.fori_loop(Z - 1, pieces, lambda u, v: (g_step(u), v)[1], 0)
+
+    def g_done(s):
+        @pl.when(z > 0)
+        def _():
+            g_p(s, z).wait_recv()
+
+        @pl.when(z < Z - 1)
+        def _():
+            g_m(s, z).wait_recv()
+
+    row = lax.broadcasted_iota(jnp.int32, (Q, Q), 0)
+    col = lax.broadcasted_iota(jnp.int32, (Q, Q), 1)
+    side = half // (NDP // NCH)
+    chan, part = row // 2, row % 2
+    split[...] = jnp.where((chan // side) * 2 * side + part * side + chan % side == col, 1.0, 0.0).astype(BF)
+    for i in range(2):
+        join[i] = jnp.where(2 * row[:half] + i == col[:half], 1.0, 0.0).astype(BF)
+
+    loop(Z, g_done)
+
+    def sum_g(m):
+        at = (m, pl.ds(z * LB, LB), slice(None))
+        put(wide, pl.ds(m * LB, LB), pg[at].astype(F32) + rgp[at].astype(F32) + rgm[at].astype(F32))
+
+    loop(M, sum_g, 2)
+
+    def flat_of(l):
+        rows = take(wide, l, M, LB)
+        flat[l, :M, :] = rows
+        flat[l, M:, :] = partner_rows(rows.astype(F32)).astype(BF)
+
+    loop(LB, flat_of, 4)
+
+    def e_copy(i):
+        return pltpu.make_async_remote_copy(
+            src_ref=flat.at[:, pl.ds(0, M)], dst_ref=e_hbm.at[d], send_sem=es_sem.at[i],
+            recv_sem=er_sem.at[d], device_id={"dp": (d + i) % NDP}, device_id_type=MESH)
+
+    def e_recv(b):
+        return pltpu.make_async_remote_copy(
+            src_ref=flat.at[:, pl.ds(0, M)], dst_ref=e_hbm.at[b], send_sem=es_sem.at[0],
+            recv_sem=er_sem.at[b], device_id={"dp": mate}, device_id_type=MESH)
+
+    e_local = pltpu.make_async_copy(flat.at[:, pl.ds(0, M)], e_hbm.at[d], el_sem.at[0])
+    e_local.start()
+
+    def t_copy(k):
+        rows = pl.ds(k * KB, KB)
+        return pltpu.make_async_remote_copy(
+            src_ref=give.at[rows], dst_ref=got.at[rows], send_sem=ts_sem.at[k],
+            recv_sem=tr_sem.at[k], device_id={"chan": other}, device_id_type=MESH)
+
+    def mix(i):
+        slot = i % WS
+        w_copy(i, slot).wait()
+
+        def one(j):
+            l = i * WL + j
+            both = flat[l]
+            give[l] = nt(both, wbuf[slot, j, pl.ds(other * half, half), :]).astype(BF)
+            keep[l] = nt(both, wbuf[slot, j, pl.ds(c * half, half), :]).astype(BF)
+
+        loop(WL, one)
+
+        @pl.when(i + WS < LB // WL)
+        def _():
+            w_copy(i + WS, slot).start()
+
+        done = (i + 1) * WL
+
+        @pl.when(done % KB == 0)
+        def _():
+            t_copy(done // KB - 1).start()
+
+    def s_step(k):
+        def body(i):
+            up, down = Z - 1 - i, i
+
+            @pl.when((up > z) & (z > 0))
+            def _():
+                s_p(k, up).wait_recv()
+                add_s(rsp, k, up)
+                s_p(k, up).start()
+
+            @pl.when((down < z) & (z < Z - 1))
+            def _():
+                s_m(k, down).wait_recv()
+                add_s(rsm, k, down)
+                s_m(k, down).start()
+
+        loop(Z - 1, body)
+
+    owners = NDP // NCH
+    piece_width = Q // owners
+
+    def p_copy(k, e, j):
+        return pltpu.make_async_remote_copy(
+            src_ref=planar.at[pl.ds(k * KB, KB), :, pl.ds(e * piece_width, piece_width)],
+            dst_ref=l_hbm.at[d, pl.ds(k * KB, KB)],
+            send_sem=ps_sem.at[k, e * NCH + j], recv_sem=pr_sem.at[k, d],
+            device_id={"dp": c * owners + e, "chan": j}, device_id_type=MESH)
+
+    def p_recv(k, b):
+        return pltpu.make_async_remote_copy(
+            src_ref=planar.at[pl.ds(k * KB, KB), :, pl.ds(0, piece_width)],
+            dst_ref=l_hbm.at[b, pl.ds(k * KB, KB)],
+            send_sem=ps_sem.at[k, 0], recv_sem=pr_sem.at[k, b],
+            device_id={"dp": mate}, device_id_type=MESH)
+
+    def p_local(k, e):
+        return pltpu.make_async_copy(
+            planar.at[pl.ds(k * KB, KB), :, pl.ds(e * piece_width, piece_width)],
+            l_hbm.at[d, pl.ds(k * KB, KB)], pl_sem.at[k])
+
+    def is_me(e, j):
+        return (d == c * owners + e) & (c == j)
+
+    def s_finish(k):
+        @pl.when(z > 0)
+        def _():
+            s_p(k, z).wait_recv()
+
+        @pl.when(z < Z - 1)
+        def _():
+            s_m(k, z).wait_recv()
+
+        def total(m):
+            at = (m, pl.ds(z * LB + k * KB, KB), slice(None))
+            put(wide, pl.ds(m * KB, KB), ps[at].astype(F32) + rsp[at].astype(F32) + rsm[at].astype(F32))
+
+        loop(M, total, 2)
+
+        def one(l):
+            rows16[pl.ds(l * M, M), :] = take(wide, l, M, KB)
+
+        loop(KB, one, 4)
+        planar[pl.ds(k * KB, KB)] = nn(rows16[...], split[...]).astype(BF).reshape(KB, M, Q)
+        for e in range(owners):
+            for j in range(NCH):
+                @pl.when(is_me(e, j))
+                def _():
+                    p_local(k, e).start()
+
+                @pl.when(jnp.logical_not(is_me(e, j)))
+                def _():
+                    p_copy(k, e, j).start()
+
+    def a_region(t, k):
+        return (slice(None), pl.ds(t * LB + k * KB, KB), slice(None))
+
+    def a_p(t, k):
+        part = spec.at[a_region(t, k)]
+        return pltpu.make_async_remote_copy(
+            src_ref=part, dst_ref=part, send_sem=aps.at[t, k], recv_sem=apr.at[t, k],
+            device_id={"lat": (z + 1) % Z}, device_id_type=MESH)
+
+    def a_m(t, k):
+        part = spec.at[a_region(t, k)]
+        return pltpu.make_async_remote_copy(
+            src_ref=part, dst_ref=part, send_sem=ams.at[t, k], recv_sem=amr.at[t, k],
+            device_id={"lat": (z + Z - 1) % Z}, device_id_type=MESH)
+
+    def combine(k):
+        t_copy(k).wait_recv()
+        rows = pl.ds(k * KB, KB)
+        total = (keep[rows].astype(F32) + got[rows].astype(F32)).astype(BF)
+        real = total[:, :M].reshape(KB * M, half)
+        imag = total[:, M:].reshape(KB * M, half)
+        put(wide, pl.ds(0, KB * M), nn(real, join[0]) + nn(imag, join[1]))
+
+        def one(m):
+            spec[m, pl.ds(z * LB + k * KB, KB), :] = take(wide, m, KB, M)
+
+        loop(M, one, 4)
+
+        @pl.when(z < Z - 1)
+        def _():
+            a_p(z, k).start()
+
+        @pl.when(z > 0)
+        def _():
+            a_m(z, k).start()
+
+    def a_step(dist):
+        def body(k):
+            below, above = z - dist, z + dist
+
+            @pl.when(below >= 0)
+            def _():
+                a_p(below, k).wait_recv()
+
+                @pl.when(z < Z - 1)
+                def _():
+                    a_p(below, k).start()
+
+            @pl.when(above < Z)
+            def _():
+                a_m(above, k).wait_recv()
+
+                @pl.when(z > 0)
+                def _():
+                    a_m(above, k).start()
+
+        loop(K, body)
+
+    def mix_rows(k):
+        lax.fori_loop(k * (KB // WL), (k + 1) * (KB // WL), lambda i, v: (mix(i), v)[1], 0)
+
+    mix_rows(0)
+    for k in range(1, K):
+        mix_rows(k)
+        combine(k - 1)
+    for i in range(1, NDP):
+        e_copy(i).start()
+    combine(K - 1)
+    for k in range(1, K):
+        s_send(k)
+    s_step(0)
+    s_finish(0)
+    todo = list(range(1, K))
+    for dist in range(1, Z):
+        a_step(dist)
+        if todo and dist < Z - 1:
+            k = todo.pop(0)
+            s_step(k)
+            s_finish(k)
+
+    def back(m):
+        put(wide, pl.ds(m, J, stride=M), tn(tall[m], spec[m]))
+
+    loop(M, back, 2)
+
+    def narrow(i):
+        at = pl.ds(i * JB, JB)
+        rows = pl.ds(i * JB * M, JB * M)
+        for q in range(Q // 128):
+            outb[at, :, q * 128:(q + 1) * 128] = wide[q, rows, :].reshape(JB, M, 128).astype(BF)
+
+    loop(J // JB, narrow)
+    out = pltpu.make_async_copy(outb, gi_hbm, out_sem.at[0])
+    out.start()
+    for k in todo:
+        s_step(k)
+        s_finish(k)
+
+    e_local.wait()
+    for i in range(1, NDP):
+        e_copy(i).wait_send()
+        e_recv((d + i) % NDP).wait_recv()
+    for k in range(K):
+        t_copy(k).wait_send()
+        for e in range(owners):
+            for j in range(NCH):
+                @pl.when(is_me(e, j))
+                def _():
+                    p_local(k, e).wait()
+
+                @pl.when(jnp.logical_not(is_me(e, j)))
+                def _():
+                    p_copy(k, e, j).wait_send()
+        for b in range(NDP):
+            @pl.when(jnp.logical_not((b == d) & (d // owners == c)))
+            def _():
+                p_recv(k, b).wait_recv()
+    for i in range(1, Z):
+        source = (z + i) % Z
+        z_copy(source, z).wait_send()
+        quarter(source, mine_q, xs_sem.at[source], xr_sem.at[source], {"chan": other}).wait_send()
+        quarter(source, mine_q, cs_sem.at[source, 0], cr_sem.at[source, 0], {"dp": mate}).wait_send()
+        quarter(source, other * 2 + core, cs_sem.at[source, 1], cr_sem.at[source, 1], {"dp": mate}).wait_send()
+
+    def drain_line(i):
+        s, t = i // Z, i % Z
+
+        @pl.when((t > z) & (z < Z - 1))
+        def _():
+            g_p(s, t).wait_send()
+
+        @pl.when((t < z) & (z > 0))
+        def _():
+            g_m(s, t).wait_send()
+
+    loop(Z * Z, drain_line)
+
+    def drain_rest(i):
+        k, t = i // Z, i % Z
+
+        @pl.when(t > z)
+        def _():
+            s_p(k, t).wait_send()
+
+        @pl.when(t < z)
+        def _():
+            s_m(k, t).wait_send()
+
+        @pl.when((t <= z) & (z < Z - 1))
+        def _():
+            a_p(t, k).wait_send()
+
+        @pl.when((t >= z) & (z > 0))
+        def _():
+            a_m(t, k).wait_send()
+
+    loop(K * Z, drain_rest)
+    out.wait()
+
+
+def weight_kernel(scale, e_ref, l_ref, out_ref):
+    n_b, n_l, m, q = e_ref.shape
+    side = l_ref.shape[-1] // 2
+
+    for l in range(n_l):
+        right = e_ref[:, l].reshape(n_b * m, q)
+        left = l_ref[:, l].reshape(n_b * m, 2 * side)
+        turned = partner_rows(right.astype(F32)).astype(BF)
+        total = tn(jnp.concatenate([left[:, :side], left[:, side:]], axis=0),
+                   jnp.concatenate([right, turned], axis=0))
+        out_ref[l] = (total * scale).astype(BF)
+
+
+def fast(saved_input, grad_output, legendre, quad_weight, mixing_weight):
+    _, M, J, Q = saved_input.shape
+    OM, L, _ = legendre.shape
+    Z, NDP, NCH = lax.axis_size("lat"), lax.axis_size("dp"), lax.axis_size("chan")
+    LB, NI, _ = mixing_weight.shape
+    KB = 16
+    K = LB // KB
+    WL, WS = 8, 3
+    half = Q // 2
+    owners = NDP // NCH
+    side = half // owners
+    dims = (J, M, Q, L, LB, OM, Z, NDP, NCH, K, KB, WL, WS)
+    quad = quad_weight.reshape(Z, J)
+    g = jnp.transpose(grad_output[0], (1, 0, 2))
+    x = jnp.transpose(saved_input[0], (1, 0, 2))
+    anyspec = pl.BlockSpec(memory_space=pl.ANY)
+    dma = pltpu.SemaphoreType.DMA
+    part_shape = pltpu.VMEM((M, L, Q), BF)
+    scratch = [
+        pltpu.VMEM((OM, L, Z * J), BF), pltpu.VMEM((Z, OM, L, J), BF), pltpu.VMEM((Z, J), F32), pltpu.VMEM((2, J, M, Q), BF),
+        pltpu.VMEM((Q // 128, J * M, 128), F32), pltpu.VMEM((M, L, J), BF),
+        part_shape, part_shape, part_shape, part_shape, part_shape, part_shape,
+        pltpu.VMEM((M, L, J), BF), pltpu.VMEM((LB, 2 * M, Q), BF),
+        pltpu.VMEM((LB, 2 * M, half), BF), pltpu.VMEM((LB, 2 * M, half), BF),
+        pltpu.VMEM((LB, 2 * M, half), BF), part_shape, pltpu.VMEM((LB, M, Q), BF),
+        pltpu.VMEM((KB * M, Q), BF),
+        pltpu.VMEM((WS, WL, NI, Q), BF), pltpu.VMEM((Q, Q), BF), pltpu.VMEM((2, half, Q), BF),
+        pltpu.VMEM((J, M, Q), BF),
+        dma((4,)), dma((WS,)), dma((Z,)), dma((Z,)), dma((Z,)), dma((Z,)), dma((Z, 2)), dma((Z, 2)),
+        dma((Z, Z)), dma((Z, Z)), dma((Z, Z)), dma((Z, Z)),
+        dma((K, Z)), dma((K, Z)), dma((K, Z)), dma((K, Z)),
+        dma((K,)), dma((K,)), dma((Z, K)), dma((Z, K)), dma((Z, K)), dma((Z, K)),
+        dma((NDP,)), dma((NDP,)), dma((1,)), dma((K, owners * NCH)), dma((K, NDP)), dma((K,)),
+        dma((1,)),
+    ]
+    gi, e, left = pl.pallas_call(
+        functools.partial(layer_kernel, dims),
+        out_shape=(
+            jax.ShapeDtypeStruct((J, M, Q), BF),
+            jax.ShapeDtypeStruct((NDP, LB, M, Q), BF),
+            jax.ShapeDtypeStruct((NDP, LB, M, 2 * side), BF),
+        ),
+        in_specs=[anyspec] * 5,
+        out_specs=(anyspec,) * 3,
+        scratch_shapes=scratch,
+        compiler_params=pltpu.CompilerParams(
+            collective_id=0, has_side_effects=True, vmem_limit_bytes=67043328
+        ),
+        name="layer",
+    )(legendre, quad, g, x, mixing_weight)
+    WB = 8
+    gw = pl.pallas_call(
+        functools.partial(weight_kernel, 1.0 / (NDP * saved_input.shape[0])),
+        out_shape=jax.ShapeDtypeStruct((LB, side, Q), BF),
+        grid=(LB // WB,),
+        in_specs=[
+            pl.BlockSpec((NDP, WB, M, Q), lambda i: (0, i, 0, 0)),
+            pl.BlockSpec((NDP, WB, M, 2 * side), lambda i: (0, i, 0, 0)),
+        ],
+        out_specs=pl.BlockSpec((WB, side, Q), lambda i: (i, 0, 0)),
+        compiler_params=pltpu.CompilerParams(dimension_semantics=("arbitrary",)),
+        name="weight",
+    )(e, left)
+    return gw, jnp.transpose(gi, (1, 0, 2))[None]
 
 
 def lane_swap(width):
@@ -132,6 +795,21 @@
     return (real + imag).astype(BF)
 
 
+def on_slice(saved_input, grad_output, legendre, quad_weight, mixing_weight):
+    n_b, n_m, n_j, width = saved_input.shape
+    own_m, n_deg, _ = legendre.shape
+    lat, n_dp, n_chan = (lax.axis_size(a) for a in ("lat", "dp", "chan"))
+    n_l, n_i, _ = mixing_weight.shape
+    fits = (
+        n_b == 1 and n_chan == 2 and n_dp % 2 == 0 and n_dp // n_chan == 2
+        and n_m == lat * own_m and n_m == 16 and own_m % (2 * n_chan) == 0
+        and n_l % 16 == 0 and n_l >= 32 and width % 512 == 0 and n_i == width
+        and n_j % 12 == 0
+    )
+    step = fast if fits else on_device
+    return step(saved_input, grad_output, legendre, quad_weight, mixing_weight)
+
+
 def solution(mesh):
     in_specs = (
         P("dp", None, "lat", "chan"),
@@ -142,5 +820,5 @@
     )
     out_specs = (P("lat", "dp", "chan"), P("dp", None, "lat", "chan"))
     return jax.shard_map(
-        on_device, mesh=mesh, in_specs=in_specs, out_specs=out_specs, check_vma=False
+        on_slice, mesh=mesh, in_specs=in_specs, out_specs=out_specs, check_vma=False
     )

time: 257 us -> 203 us (0.79)
  Pallas kernels: 0 us -> 199 us
  waiting for transfers between devices: 120 us -> 0 us
  matrix products: 55.3 us -> 0 us
  blocking collectives: 21.7 us -> 0 us
  local copies, waits for them, and re-layouts: 22.2 us -> 2.96 us
  other arithmetic: 13.9 us -> 0 us
  between operations: 14 us -> 0.65 us
  starting transfers between devices: 9.19 us -> 0 us
    pallas_call x0 -> x2, Pallas kernels: none -> 199 us  [the longest x1 191 us: fast(): pl.pallas_call(functools.partial(layer_kernel, dims), out_shape=(jax.Shap...]
    reduce_scatter x2 -> x0, waiting for transfers between devices: 73.7 us -> none  [spectrum(): lax.psum_scatter(part.astype(BF), 'lat', scatter_dimension=0, tiled=True)]
    dot_general x10 -> x0, matrix products: 55.3 us -> none  [the longest x1 13.5 us: on_device(): jnp.einsum('dtlrpi,pdlrq->ltiq', left, right, preferred_element_type=F32)]
    ppermute x9 -> x0, waiting for transfers between devices: 39.6 us -> none  [the longest x8 37.3 us: shifted(): return lax.ppermute(x, axis, [(i, (i + step) % n) for i in range(n)])]
    all_to_all x1 -> x0, blocking collectives: 21.7 us -> none  [on_device(): lax.all_to_all(by_lat, 'lat', split_axis=0, concat_axis=0, tiled=True)]
    ppermute x9 -> x0, starting transfers between devices: 8.88 us -> none  [the longest x8 8.88 us: shifted(): return lax.ppermute(x, axis, [(i, (i + step) % n) for i in range(n)])]
    reshape x6 -> x1, local copies, waits for them, and re-layouts: 8.64 us -> 1.36 us  [fast(): quad = quad_weight.reshape(Z, J)]
    all_gather x1 -> x0, waiting for transfers between devices: 6.61 us -> none  [on_device(): lax.all_gather(half, 'lat', axis=0, tiled=True).reshape(-1, n_b, n_m, width)]
  transfers between devices with their start and end apart: 12 -> 0, of which waited for: 9 -> 0; matrix products, arithmetic and copies ran while one was open for 23% -> 0% of each run, Pallas kernels for 0% -> 0%
where the time goes in v1:
time: 203 us
  Pallas kernels  199 us (98%)
  local copies, waits for them, and re-layouts  2.96 us (1%)
    pallas_call x1, Pallas kernels, fast(): pl.pallas_call(functools.partial(layer_kernel, dims), out_shape=(jax.Shap...  191 us
    pallas_call x1, Pallas kernels, fast(): pl.pallas_call(functools.partial(weight_kernel, 1.0 / (NDP * saved_input....  8.39 us

profile of v1, /device:TPU:0, one launch (start us, length us, event | category | flops | bytes accessed | tf_op | source)
XLA Modules:
  0.0 202.6 jit_solution(17709851193747134041)
XLA Ops:
  0.6 1.4 reshape.7.quad_hbm
  2.0 190.6 %layer.1 = (bf16[180,16,512]{2,1,0:T(8,128)(2,1)}, bf16[4,48,16,512]{3,2,1,0:T(8,128)(2,1)}, bf16[4,48,16,256]{3,2,1,0:T(8,128)(2,1)}) custom-call(bf16[4,192,720]{2,1,0:T(8,128)(2,1)} %leg_hbm.1, f32[4,180]{1,0:T(4,128)} %reshape.7.quad_hbm, bf16[180,16,512]{2,1,0:T(8,128)(2,1)} %bitcast.9, bf16[180,16,512]{2,1,0:T(8,128)(2,1)} %bitcast.10, ...), custom_call_target="tpu_custom_call" | custom-call | tf_op jit(solution)/shard_map/layer/pallas_call | solution.py:642
  192.6 0.0 copy-start
  192.6 8.4 %weight.1 = bf16[48,128,512]{2,1,0:T(8,128)(2,1)} custom-call(bf16[4,48,16,512]{3,2,1,0:T(8,128)(2,1)} %get-tuple-element.5.e_ref, bf16[4,48,16,256]{3,2,1,0:T(8,128)(2,1)} %get-tuple-element.6.l_ref), custom_call_target="tpu_custom_call" | custom-call | tf_op jit(solution)/shard_map/weight/pallas_call | solution.py:658
  201.0 0.0 copy-done
  201.0 1.6 copy.8
Async XLA Ops:
  192.6 8.4 %copy-start = (bf16[180,16,512]{2,1,0:T(8,128)(2,1)S(1)}, bf16[180,16,512]{2,1,0:T(8,128)(2,1)}, u32[]{:S(2)}) copy-start(bf16[180,16,512]{2,1,0:T(8,128)(2,1)} %get-tuple-element.7) | copy-start | bytes 8847364

commit v2 on v1

--- a/solution.py
+++ b/solution.py
@@ -11,6 +11,10 @@
 MESH = pl.DeviceIdType.MESH
 
 
+START = 0
+DELAY = 3
+
+
 def loop(n, body, unroll=1):
     if n % unroll:
         unroll = 1
@@ -56,7 +60,7 @@
     dims,
     leg_hbm, quad_hbm, g_hbm, x_hbm, w_hbm,
     gi_hbm, e_hbm, l_hbm,
-    leg, tab, quad, raw, wide, table, pg, ps, rgp, rgm, rsp, rsm,
+    leg, tab, quad_in, quad, raw, wide, table, pg, ps, rgp, rgm, rsp, rsm,
     tall, flat, keep, give, got, spec, planar, rows16, wbuf, split, join, outb,
     load_sem, w_sem, zs_sem, zr_sem, xs_sem, xr_sem, cs_sem, cr_sem,
     gps, gpr, gms, gmr, sps, spr, sms, smr,
@@ -73,9 +77,9 @@
         return pltpu.make_async_copy(src, dst, load_sem.at[i])
 
     loads = [load(leg_hbm, leg, 0), load(g_hbm, raw.at[0], 1), load(x_hbm, raw.at[1], 2),
-             load(quad_hbm, quad, 3)]
-    for copy in loads:
-        copy.start()
+             load(quad_hbm, quad_in, 3)]
+    for i in (0, 1, 3, 2):
+        loads[i].start()
 
     def w_copy(i, slot):
         return pltpu.make_async_copy(w_hbm.at[pl.ds(i * WL, WL)], wbuf.at[slot], w_sem.at[slot])
@@ -184,12 +188,12 @@
 
     @pl.when(first)
     def _():
-        for t in range(Z - 1, 0, -1):
+        for t in [*range(Z - 2, 0, -1), Z - 1]:
             g_p(0, t).start()
 
     @pl.when(last)
     def _():
-        for t in range(Z - 1):
+        for t in [*range(1, Z - 1), 0]:
             g_m(Z - 1, t).start()
 
     for i in range(1, Z):
@@ -226,7 +230,11 @@
     def order(u):
         v = u - (Z - 1)
         early = u < Z - 1
-        return jnp.where(early, 0, 1 + v % (Z - 1)), jnp.where(early, Z - 1 - u, Z - 1 - v // (Z - 1))
+        p = jnp.where(early, u, v // (Z - 1))
+        return jnp.where(early, 0, 1 + v % (Z - 1)), jnp.where(p < Z - 2, Z - 2 - p, Z - 1)
+
+    def down_block(t):
+        return Z - 1 - t
 
     pieces = Z * (Z - 1)
 
@@ -239,30 +247,16 @@
 
         @pl.when(last)
         def _():
-            g_m(Z - 1 - s, Z - 1 - t).start()
+            g_m(Z - 1 - s, down_block(t)).start()
 
     lax.fori_loop(Z - 1, pieces, lambda u, v: (g_ends(u), v)[1], 0)
-
-    def g_step(u):
-        s, t = order(u)
-        back, low = Z - 1 - s, Z - 1 - t
-
-        @pl.when((z > 0) & (t > z))
-        def _():
-            g_p(s, t).wait_recv()
-            add_g(rgp, s, t)
-            g_p(s, t).start()
-
-        @pl.when((z < Z - 1) & (low < z))
-        def _():
-            g_m(back, low).wait_recv()
-            add_g(rgm, back, low)
-            g_m(back, low).start()
-
-    loop(Z - 1, g_step)
 
     loads[2].wait()
     loads[3].wait()
+    weights = quad_in[...].reshape(1, Z * J)
+    for t in range(Z):
+        quad[t:t + 1, :] = weights[:, t * J:(t + 1) * J]
+
     spread(1)
 
     def input_part(m):
@@ -282,8 +276,8 @@
             for t in range(Z - 1):
                 s_m(k, t).start()
 
-    s_send(0)
-    lax.fori_loop(Z - 1, pieces, lambda u, v: (g_step(u), v)[1], 0)
+    for k in range(K - 1):
+        s_send(k)
 
     def g_done(s):
         @pl.when(z > 0)
@@ -302,20 +296,16 @@
     for i in range(2):
         join[i] = jnp.where(2 * row[:half] + i == col[:half], 1.0, 0.0).astype(BF)
 
-    loop(Z, g_done)
-
     def sum_g(m):
         at = (m, pl.ds(z * LB, LB), slice(None))
         put(wide, pl.ds(m * LB, LB), pg[at].astype(F32) + rgp[at].astype(F32) + rgm[at].astype(F32))
 
-    loop(M, sum_g, 2)
 
     def flat_of(l):
         rows = take(wide, l, M, LB)
         flat[l, :M, :] = rows
         flat[l, M:, :] = partner_rows(rows.astype(F32)).astype(BF)
 
-    loop(LB, flat_of, 4)
 
     def e_copy(i):
         return pltpu.make_async_remote_copy(
@@ -328,7 +318,14 @@
             recv_sem=er_sem.at[b], device_id={"dp": mate}, device_id_type=MESH)
 
     e_local = pltpu.make_async_copy(flat.at[:, pl.ds(0, M)], e_hbm.at[d], el_sem.at[0])
-    e_local.start()
+
+    def own_spectra():
+        loop(Z, g_done)
+        loop(M, sum_g, 2)
+        loop(LB, flat_of, 4)
+        e_local.start()
+        for i in range(1, NDP):
+            e_copy(i).start()
 
     def t_copy(k):
         rows = pl.ds(k * KB, KB)
@@ -357,24 +354,6 @@
         @pl.when(done % KB == 0)
         def _():
             t_copy(done // KB - 1).start()
-
-    def s_step(k):
-        def body(i):
-            up, down = Z - 1 - i, i
-
-            @pl.when((up > z) & (z > 0))
-            def _():
-                s_p(k, up).wait_recv()
-                add_s(rsp, k, up)
-                s_p(k, up).start()
-
-            @pl.when((down < z) & (z < Z - 1))
-            def _():
-                s_m(k, down).wait_recv()
-                add_s(rsm, k, down)
-                s_m(k, down).start()
-
-        loop(Z - 1, body)
 
     owners = NDP // NCH
     piece_width = Q // owners
@@ -467,49 +446,141 @@
         def _():
             a_m(z, k).start()
 
-    def a_step(dist):
-        def body(k):
-            below, above = z - dist, z + dist
-
-            @pl.when(below >= 0)
-            def _():
-                a_p(below, k).wait_recv()
-
-                @pl.when(z < Z - 1)
-                def _():
-                    a_p(below, k).start()
-
-            @pl.when(above < Z)
-            def _():
-                a_m(above, k).wait_recv()
-
-                @pl.when(z > 0)
-                def _():
-                    a_m(above, k).start()
-
-        loop(K, body)
+        @pl.when(k == K - 1)
+        def _():
+            s_send(K - 1)
 
     def mix_rows(k):
         lax.fori_loop(k * (KB // WL), (k + 1) * (KB // WL), lambda i, v: (mix(i), v)[1], 0)
 
-    mix_rows(0)
-    for k in range(1, K):
-        mix_rows(k)
-        combine(k - 1)
-    for i in range(1, NDP):
-        e_copy(i).start()
-    combine(K - 1)
-    for k in range(1, K):
-        s_send(k)
-    s_step(0)
-    s_finish(0)
-    todo = list(range(1, K))
-    for dist in range(1, Z):
-        a_step(dist)
-        if todo and dist < Z - 1:
-            k = todo.pop(0)
-            s_step(k)
-            s_finish(k)
+    s_count = (K - 1) * (Z - 1)
+    gather_at = pieces + s_count
+    final_at = gather_at + K
+    total_pieces = final_at + Z - 1
+
+    def up(n):
+        @pl.when((n >= 0) & (n < pieces))
+        def _():
+            s, t = order(n)
+
+            @pl.when(t > z)
+            def _():
+                g_p(s, t).wait_recv()
+                add_g(rgp, s, t)
+                g_p(s, t).start()
+
+        late = n >= final_at
+
+        @pl.when(((n >= pieces) & (n < gather_at)) | (late & (n < total_pieces)))
+        def _():
+            v = jnp.where(late, n - final_at + s_count, n - pieces)
+            k, t = v // (Z - 1), Z - 1 - v % (Z - 1)
+
+            @pl.when(t > z)
+            def _():
+                s_p(k, t).wait_recv()
+                add_s(rsp, k, t)
+                s_p(k, t).start()
+
+        @pl.when((n >= gather_at) & (n < final_at))
+        def _():
+            a_p(0, n - gather_at).wait_recv()
+            a_p(0, n - gather_at).start()
+
+    def down(n):
+        @pl.when((n >= 0) & (n < pieces))
+        def _():
+            s, t = order(n)
+            s, t = Z - 1 - s, down_block(t)
+
+            @pl.when(t < z)
+            def _():
+                g_m(s, t).wait_recv()
+                add_g(rgm, s, t)
+                g_m(s, t).start()
+
+        late = n >= final_at
+
+        @pl.when(((n >= pieces) & (n < gather_at)) | (late & (n < total_pieces)))
+        def _():
+            v = jnp.where(late, n - final_at + s_count, n - pieces)
+            k, t = v // (Z - 1), v % (Z - 1)
+
+            @pl.when(t < z)
+            def _():
+                s_m(k, t).wait_recv()
+                add_s(rsm, k, t)
+                s_m(k, t).start()
+
+        @pl.when((n >= gather_at) & (n < final_at))
+        def _():
+            a_m(Z - 1, n - gather_at).wait_recv()
+            a_m(Z - 1, n - gather_at).start()
+
+    inner = jnp.logical_not(first | last)
+    begin = (Z - 1) * (Z - 1) + START - 1
+    ready = [pieces + (k + 1) * (Z - 1) + 1 for k in range(K - 1)]
+
+    def slot(v):
+        @pl.when(inner)
+        def _():
+            up(v - (z - 1))
+            down(v - (Z - 2 - z))
+
+        u = v - begin
+
+        @pl.when(u == 0)
+        def _():
+            own_spectra()
+
+        @pl.when((u >= 1) & (u < K + 1))
+        def _():
+            mix_rows(u - 1)
+
+        @pl.when((u >= K) & (u < 2 * K))
+        def _():
+            combine(u - K)
+
+        for b in range(1, Z - 1):
+            @pl.when((b < z) & inner)
+            def _():
+                w = v - begin - (K - 1) - DELAY * (z - b)
+
+                @pl.when((w >= 0) & (w < K))
+                def _():
+                    a_p(b, w).wait_recv()
+                    a_p(b, w).start()
+
+            @pl.when((b > z) & inner)
+            def _():
+                w = v - begin - (K - 1) - DELAY * (b - z)
+
+                @pl.when((w >= 0) & (w < K))
+                def _():
+                    a_m(b, w).wait_recv()
+                    a_m(b, w).start()
+
+        hit = functools.reduce(lambda a, b: a | b, [v == r for r in ready])
+
+        @pl.when(hit)
+        def _():
+            s_finish((v - ready[0]) // (Z - 1))
+
+    loop(total_pieces + Z - 2, slot)
+
+    def collect(i):
+        b, k = i // K, i % K
+
+        @pl.when(last & (b < Z - 1))
+        def _():
+            a_p(b, k).wait_recv()
+
+        @pl.when(first & (b > 0))
+        def _():
+            a_m(b, k).wait_recv()
+
+    s_finish(K - 1)
+    loop(Z * K, collect)
 
     def back(m):
         put(wide, pl.ds(m, J, stride=M), tn(tall[m], spec[m]))
@@ -525,10 +596,6 @@
     loop(J // JB, narrow)
     out = pltpu.make_async_copy(outb, gi_hbm, out_sem.at[0])
     out.start()
-    for k in todo:
-        s_step(k)
-        s_finish(k)
-
     e_local.wait()
     for i in range(1, NDP):
         e_copy(i).wait_send()
@@ -616,14 +683,14 @@
     owners = NDP // NCH
     side = half // owners
     dims = (J, M, Q, L, LB, OM, Z, NDP, NCH, K, KB, WL, WS)
-    quad = quad_weight.reshape(Z, J)
+    quad = quad_weight
     g = jnp.transpose(grad_output[0], (1, 0, 2))
     x = jnp.transpose(saved_input[0], (1, 0, 2))
     anyspec = pl.BlockSpec(memory_space=pl.ANY)
     dma = pltpu.SemaphoreType.DMA
     part_shape = pltpu.VMEM((M, L, Q), BF)
     scratch = [
-        pltpu.VMEM((OM, L, Z * J), BF), pltpu.VMEM((Z, OM, L, J), BF), pltpu.VMEM((Z, J), F32), pltpu.VMEM((2, J, M, Q), BF),
+        pltpu.VMEM((OM, L, Z * J), BF), pltpu.VMEM((Z, OM, L, J), BF), pltpu.VMEM((Z * J,), F32), pltpu.VMEM((Z, J), F32), pltpu.VMEM((2, J, M, Q), BF),
         pltpu.VMEM((Q // 128, J * M, 128), F32), pltpu.VMEM((M, L, J), BF),
         part_shape, part_shape, part_shape, part_shape, part_shape, part_shape,
         pltpu.VMEM((M, L, J), BF), pltpu.VMEM((LB, 2 * M, Q), BF),

time: 203 us -> 166 us (0.82)
  Pallas kernels: 199 us -> 163 us
    pallas_call x1, Pallas kernels: 191 us -> 155 us  [fast(): pl.pallas_call(functools.partial(layer_kernel, dims), out_shape=(jax.Shap...]
where the time goes in v2:
time: 166 us
  Pallas kernels  163 us (98%)
    pallas_call x1, Pallas kernels, fast(): pl.pallas_call(functools.partial(layer_kernel, dims), out_shape=(jax.Shap...  155 us
    pallas_call x1, Pallas kernels, fast(): pl.pallas_call(functools.partial(weight_kernel, 1.0 / (NDP * saved_input....  8.38 us

profile of v2, /device:TPU:0, one launch (start us, length us, event | category | flops | bytes accessed | tf_op | source)
XLA Modules:
  0.0 165.7 jit_solution(309185970399212661)
XLA Ops:
  0.6 155.1 %layer.1 = (bf16[180,16,512]{2,1,0:T(8,128)(2,1)}, bf16[4,48,16,512]{3,2,1,0:T(8,128)(2,1)}, bf16[4,48,16,256]{3,2,1,0:T(8,128)(2,1)}) custom-call(bf16[4,192,720]{2,1,0:T(8,128)(2,1)} %leg_hbm.1, f32[720]{0:T(1024)} %quad_hbm.1, bf16[180,16,512]{2,1,0:T(8,128)(2,1)} %bitcast.9, bf16[180,16,512]{2,1,0:T(8,128)(2,1)} %bitcast.10, bf16[48,512,512]{2,1,0:T(8,128)(2,1)} %w_hbm.1), custom_call_target="tpu_custom_call" | custom-call | tf_op jit(solution)/shard_map/layer/pallas_call | solution.py:709
  155.7 0.0 copy-start
  155.7 8.4 %weight.1 = bf16[48,128,512]{2,1,0:T(8,128)(2,1)} custom-call(bf16[4,48,16,512]{3,2,1,0:T(8,128)(2,1)} %get-tuple-element.5.e_ref, bf16[4,48,16,256]{3,2,1,0:T(8,128)(2,1)} %get-tuple-element.6.l_ref), custom_call_target="tpu_custom_call" | custom-call | tf_op jit(solution)/shard_map/weight/pallas_call | solution.py:725
  164.1 0.0 copy-done
  164.1 1.6 copy.8
Async XLA Ops:
  155.7 8.4 %copy-start = (bf16[180,16,512]{2,1,0:T(8,128)(2,1)S(1)}, bf16[180,16,512]{2,1,0:T(8,128)(2,1)}, u32[]{:S(2)}) copy-start(bf16[180,16,512]{2,1,0:T(8,128)(2,1)} %get-tuple-element.7) | copy-start | bytes 8847364

commit v3 on v2

--- a/solution.py
+++ b/solution.py
@@ -61,7 +61,7 @@
     leg_hbm, quad_hbm, g_hbm, x_hbm, w_hbm,
     gi_hbm, e_hbm, l_hbm,
     leg, tab, quad_in, quad, raw, wide, table, pg, ps, rgp, rgm, rsp, rsm,
-    tall, flat, keep, give, got, spec, planar, rows16, wbuf, split, join, outb,
+    tall, turned, flat, keep, give, got, spec, planar, rows16, wbuf, split, join, outb,
     load_sem, w_sem, zs_sem, zr_sem, xs_sem, xr_sem, cs_sem, cr_sem,
     gps, gpr, gms, gmr, sps, spr, sms, smr,
     ts_sem, tr_sem, aps, apr, ams, amr, es_sem, er_sem, el_sem, ps_sem, pr_sem, pl_sem, out_sem,
@@ -196,21 +196,31 @@
         for t in [*range(1, Z - 1), 0]:
             g_m(Z - 1, t).start()
 
-    for i in range(1, Z):
+    def from_line(i):
         source = (z + i) % Z
         z_copy(z, source).wait_recv()
         quarter(source, mine_q, xs_sem.at[source], xr_sem.at[source], {"chan": other}).start()
         quarter(source, mine_q, cs_sem.at[source, 0], cr_sem.at[source, 0], {"dp": mate}).start()
-    for i in range(1, Z):
+
+    def from_side(i):
         source = (z + i) % Z
         x_q = other * 2 + core
         quarter(source, x_q, xs_sem.at[source], xr_sem.at[source], {"chan": other}).wait_recv()
         quarter(source, x_q, cs_sem.at[source, 1], cr_sem.at[source, 1], {"dp": mate}).start()
-    for i in range(1, Z):
+
+    def from_mate(i):
         source = (z + i) % Z
         quarter(source, c * 2 + 1 - core, cs_sem.at[source, 0], cr_sem.at[source, 0], {"dp": mate}).wait_recv()
         quarter(source, other * 2 + 1 - core, cs_sem.at[source, 1], cr_sem.at[source, 1], {"dp": mate}).wait_recv()
-        loop(OM, lambda i: grad_part(source * OM + i))
+        loop(OM, lambda m: grad_part(source * OM + m))
+
+    for i in range(1, Z + 2):
+        if i < Z:
+            from_line(i)
+        if 1 < i < Z + 1:
+            from_side(i - 1)
+        if i > 2:
+            from_mate(i - 2)
 
     def clear(r):
         def body(i):
@@ -519,27 +529,50 @@
 
     inner = jnp.logical_not(first | last)
     begin = (Z - 1) * (Z - 1) + START - 1
-    ready = [pieces + (k + 1) * (Z - 1) + 1 for k in range(K - 1)]
+    ready = [pieces + (k + 1) * (Z - 1) + 2 for k in range(K - 1)]
+
+    low_half, high_half = inner & (2 * z < Z - 1), inner & (2 * z >= Z - 1)
+    turn = begin + K + 2
+
+    def flip(m):
+        turned[m] = tall[m].T
 
     def slot(v):
-        @pl.when(inner)
+        u = v - begin
+
+        @pl.when(u == 0)
+        def _():
+            own_spectra()
+
+        @pl.when((u >= 1) & (u < K + 1))
+        def _():
+            mix_rows(u - 1)
+
+        @pl.when(u == K + 2)
+        def _():
+            combine(K - 1)
+
+        early = v < turn
+
+        @pl.when(low_half & early)
+        def _():
+            down(v - (Z - 2 - z))
+
+        @pl.when(high_half & early)
         def _():
             up(v - (z - 1))
+
+        @pl.when(u == K + 1)
+        def _():
+            loop(K - 1, combine)
+
+        @pl.when(low_half)
+        def _():
+            up(v - (z - 1))
+
+        @pl.when(high_half)
+        def _():
             down(v - (Z - 2 - z))
-
-        u = v - begin
-
-        @pl.when(u == 0)
-        def _():
-            own_spectra()
-
-        @pl.when((u >= 1) & (u < K + 1))
-        def _():
-            mix_rows(u - 1)
-
-        @pl.when((u >= K) & (u < 2 * K))
-        def _():
-            combine(u - K)
 
         for b in range(1, Z - 1):
             @pl.when((b < z) & inner)
@@ -560,13 +593,25 @@
                     a_m(b, w).wait_recv()
                     a_m(b, w).start()
 
+        @pl.when(low_half & (v > turn))
+        def _():
+            down(v - 1 - (Z - 2 - z))
+
+        @pl.when(high_half & (v > turn))
+        def _():
+            up(v - 1 - (z - 1))
+
+        @pl.when(v == begin + K + 3)
+        def _():
+            loop(M, flip, 2)
+
         hit = functools.reduce(lambda a, b: a | b, [v == r for r in ready])
 
         @pl.when(hit)
         def _():
             s_finish((v - ready[0]) // (Z - 1))
 
-    loop(total_pieces + Z - 2, slot)
+    loop(total_pieces + Z - 1, slot)
 
     def collect(i):
         b, k = i // K, i % K
@@ -583,7 +628,7 @@
     loop(Z * K, collect)
 
     def back(m):
-        put(wide, pl.ds(m, J, stride=M), tn(tall[m], spec[m]))
+        put(wide, pl.ds(m, J, stride=M), nn(turned[m], spec[m]))
 
     loop(M, back, 2)
 
@@ -593,9 +638,16 @@
         for q in range(Q // 128):
             outb[at, :, q * 128:(q + 1) * 128] = wide[q, rows, :].reshape(JB, M, 128).astype(BF)
 
-    loop(J // JB, narrow)
-    out = pltpu.make_async_copy(outb, gi_hbm, out_sem.at[0])
-    out.start()
+    parts = 3 if J % (3 * JB) == 0 else 1
+
+    def out(i):
+        rows = pl.ds(i * (J // parts), J // parts)
+        return pltpu.make_async_copy(outb.at[rows], gi_hbm.at[rows], out_sem.at[i])
+
+    for i in range(parts):
+        each = J // JB // parts
+        lax.fori_loop(i * each, (i + 1) * each, lambda j, v: (narrow(j), v)[1], 0)
+        out(i).start()
     e_local.wait()
     for i in range(1, NDP):
         e_copy(i).wait_send()
@@ -655,7 +707,8 @@
             a_m(t, k).wait_send()
 
     loop(K * Z, drain_rest)
-    out.wait()
+    for i in range(parts):
+        out(i).wait()
 
 
 def weight_kernel(scale, e_ref, l_ref, out_ref):
@@ -693,7 +746,7 @@
         pltpu.VMEM((OM, L, Z * J), BF), pltpu.VMEM((Z, OM, L, J), BF), pltpu.VMEM((Z * J,), F32), pltpu.VMEM((Z, J), F32), pltpu.VMEM((2, J, M, Q), BF),
         pltpu.VMEM((Q // 128, J * M, 128), F32), pltpu.VMEM((M, L, J), BF),
         part_shape, part_shape, part_shape, part_shape, part_shape, part_shape,
-        pltpu.VMEM((M, L, J), BF), pltpu.VMEM((LB, 2 * M, Q), BF),
+        pltpu.VMEM((M, L, J), BF), pltpu.VMEM((M, J, L), BF), pltpu.VMEM((LB, 2 * M, Q), BF),
         pltpu.VMEM((LB, 2 * M, half), BF), pltpu.VMEM((LB, 2 * M, half), BF),
         pltpu.VMEM((LB, 2 * M, half), BF), part_shape, pltpu.VMEM((LB, M, Q), BF),
         pltpu.VMEM((KB * M, Q), BF),
@@ -704,7 +757,7 @@
         dma((K, Z)), dma((K, Z)), dma((K, Z)), dma((K, Z)),
         dma((K,)), dma((K,)), dma((Z, K)), dma((Z, K)), dma((Z, K)), dma((Z, K)),
         dma((NDP,)), dma((NDP,)), dma((1,)), dma((K, owners * NCH)), dma((K, NDP)), dma((K,)),
-        dma((1,)),
+        dma((3,)),
     ]
     gi, e, left = pl.pallas_call(
         functools.partial(layer_kernel, dims),
@@ -721,7 +774,7 @@
         ),
         name="layer",
     )(legendre, quad, g, x, mixing_weight)
-    WB = 8
+    WB = 16
     gw = pl.pallas_call(
         functools.partial(weight_kernel, 1.0 / (NDP * saved_input.shape[0])),
         out_shape=jax.ShapeDtypeStruct((LB, side, Q), BF),

time: 166 us -> 164 us (0.988)
  no operation moved by 1% of the time
where the time goes in v3:
time: 164 us
  Pallas kernels  162 us (99%)
    pallas_call x1, Pallas kernels, fast(): pl.pallas_call(functools.partial(layer_kernel, dims), out_shape=(jax.Shap...  154 us
    pallas_call x1, Pallas kernels, fast(): pl.pallas_call(functools.partial(weight_kernel, 1.0 / (NDP * saved_input....  7.76 us

profile of v3, /device:TPU:0, one launch (start us, length us, event | category | flops | bytes accessed | tf_op | source)
XLA Modules:
  0.0 163.9 jit_solution(13046421502156423693)
XLA Ops:
  0.6 153.9 %layer.1 = (bf16[180,16,512]{2,1,0:T(8,128)(2,1)}, bf16[4,48,16,512]{3,2,1,0:T(8,128)(2,1)}, bf16[4,48,16,256]{3,2,1,0:T(8,128)(2,1)}) custom-call(bf16[4,192,720]{2,1,0:T(8,128)(2,1)} %leg_hbm.1, f32[720]{0:T(1024)} %quad_hbm.1, bf16[180,16,512]{2,1,0:T(8,128)(2,1)} %bitcast.9, bf16[180,16,512]{2,1,0:T(8,128)(2,1)} %bitcast.10, bf16[48,512,512]{2,1,0:T(8,128)(2,1)} %w_hbm.1), custom_call_target="tpu_custom_call" | custom-call | tf_op jit(solution)/shard_map/layer/pallas_call | solution.py:762
  154.6 0.0 copy-start
  154.6 7.8 %weight.1 = bf16[48,128,512]{2,1,0:T(8,128)(2,1)} custom-call(bf16[4,48,16,512]{3,2,1,0:T(8,128)(2,1)} %get-tuple-element.5.e_ref, bf16[4,48,16,256]{3,2,1,0:T(8,128)(2,1)} %get-tuple-element.6.l_ref), custom_call_target="tpu_custom_call" | custom-call | tf_op jit(solution)/shard_map/weight/pallas_call | solution.py:778
  162.3 0.0 copy-done
  162.3 1.6 copy.8
Async XLA Ops:
  154.6 7.8 %copy-start = (bf16[180,16,512]{2,1,0:T(8,128)(2,1)S(1)}, bf16[180,16,512]{2,1,0:T(8,128)(2,1)}, u32[]{:S(2)}) copy-start(bf16[180,16,512]{2,1,0:T(8,128)(2,1)} %get-tuple-element.7) | copy-start | bytes 8847364
